TPU v7x, 32 devices: a whole 2x2x4 slice. The times are simulated.
32 devices in a mesh: expert: 8 (over y, x, core), dp: 4 (over z).
Axes of the slice: x: 2, y: 2, z: 4, core: 2. Of those that a mesh axis runs over, the one named last changes fastest.
Arguments:
- gradient: bfloat16 [4, 1, 14336, 2048], P('dp', None, None, 'expert'), may hold values from -6 to 6
- momentum: float32 [4, 1, 14336, 2048], P('dp', None, 'expert'), may hold values from -6 to 6
- group_index: int32 [224, 32, 4, 32], P('expert'), may hold values from 0 to 4095, all different within a row
Outputs:
- momentum_next: float32 [4, 1, 14336, 2048], P('dp', None, 'expert')
- update: float32 [1, 14336, 2048], P(None, None, 'expert')
Inputs may be any that keep to these rules, and one draw needn't show every extreme that they name: `group_index`: an entry names the coefficient at row frequency (entry // 64) and column frequency (entry % 64) of its block; the 32 entries of one block and replica differ.
All inputs are finite; a program needn't handle non-finite values.
Results may differ from a plain program's by a relative error of at most 0.0003.
Values may be sent and summed in bfloat16 or wider, within the bound.
No kernel may reach another device: no remote copies, remote signals or barrier semaphores. Data moves between devices by JAX's collectives and lax.ppermute only.
A program may use at most 192 MiB of HBM per device.

v0:
```python
import math

import jax
import jax.numpy as jnp
from jax import lax
from jax.sharding import PartitionSpec as P

SPAN = 64


MOMENTUM_DECAY = 0.999
HIGHEST_PRECISION = lax.Precision.HIGHEST


def cosine_table(order_size):
    frequency = jnp.arange(order_size, dtype=jnp.float32)[:, None]
    position = jnp.arange(order_size, dtype=jnp.float32)[None, :]
    weighting = jnp.where(frequency == 0, math.sqrt(1.0 / order_size), math.sqrt(2.0 / order_size))
    return weighting * jnp.cos(math.pi * (2.0 * position + 1.0) * frequency / (2.0 * order_size))


def forward(blocks, cosine):
    return jnp.einsum("ui,piqj,vj->pquv", cosine, blocks, cosine, precision=HIGHEST_PRECISION)


def inverse(coeffs, cosine):
    return jnp.einsum("ui,pquv,vj->piqj", cosine, coeffs, cosine, precision=HIGHEST_PRECISION)


def place(values, picked, total):
    count_rows = picked.shape[0]
    count_cols = picked.shape[1]
    row_ids = jnp.arange(count_rows, dtype=jnp.int32)[:, None, None]
    col_ids = jnp.arange(count_cols, dtype=jnp.int32)[None, :, None]
    empty = jnp.zeros((count_rows, count_cols, total), jnp.float32)
    return empty.at[row_ids, col_ids, picked].add(values)


def on_device(gradient, momentum, group_index):
    cosine = cosine_table(SPAN)
    replica = lax.axis_index("dp")
    shifted = lax.all_to_all(gradient, "expert", split_axis=2, concat_axis=3, tiled=True)
    row_count = shifted.shape[1] * shifted.shape[2]
    col_count = shifted.shape[3]
    decayed = MOMENTUM_DECAY * momentum.reshape(row_count, col_count) + shifted.reshape(
        row_count, col_count
    ).astype(jnp.float32)
    block_rows = row_count // SPAN
    block_cols = col_count // SPAN
    blocks = decayed.reshape(block_rows, SPAN, block_cols, SPAN)
    coeffs = forward(blocks, cosine).reshape(block_rows, block_cols, SPAN * SPAN)
    own = lax.dynamic_index_in_dim(group_index, replica, 2, keepdims=False)
    values = jnp.take_along_axis(coeffs, own, axis=2)
    selected = place(values, own, SPAN * SPAN).reshape(block_rows, block_cols, SPAN, SPAN)
    restored = inverse(selected, cosine).reshape(row_count, col_count)
    momentum_next = (decayed - restored).reshape(momentum.shape)
    total = lax.psum(restored, "dp")
    update = lax.all_to_all(total[None], "expert", split_axis=2, concat_axis=1, tiled=True)
    return (momentum_next, update)


def solution(mesh):
    placed = (
        P("dp", None, None, "expert"),
        P("dp", None, "expert", None),
        P("expert", None, None, None),
    )
    return jax.shard_map(
        on_device,
        mesh=mesh,
        in_specs=placed,
        out_specs=(P("dp", None, "expert", None), P(None, None, "expert")),
        check_vma=False,
    )
```

profile of v0, /device:TPU:0, one launch (start us, length us, event | category | flops | bytes accessed | tf_op | source)
XLA Modules:
  0.0 1792.0 jit_solution(7726705985942069426)
XLA Ops:
  7.2 0.0 copy-start
  7.2 13.9 copy.47
  21.1 0.5 broadcast.103
  21.6 74.4 %reduce.4 = bf16[14336,256]{1,0:T(8,128)(2,1)} reduce(bf16[14336,1,1,256]{3,2,1,0:T(2,128)(2,1)} %bitcast.50, bf16[]{:T(256)} %broadcast.103), dimensions={1,2}, to_apply=%bitcast.46.reduce_sub_computation | reduce | bytes 14680066
  96.0 0.0 copy-start.9
  96.0 0.0 copy-start.8
  96.0 9.0 reshape.130
  105.1 5.2 all-to-all-start
  110.3 0.3 all-reduce.2.cloned.1.call-start
  110.6 0.0 copy-done
  110.6 0.5 constant_dynamic-slice_fusion
  111.1 0.0 copy-start.2
  111.1 0.8 copy-done.2
  111.9 0.2 shift-left_or_fusion
  112.2 0.0 copy-done.9
  112.2 0.3 multiply_reduce_fusion
  112.4 0.0 copy-done.8
  112.4 0.4 and_reduce_fusion
  112.8 0.1 broadcast_select_fusion
  112.9 0.8 reshape.121
  113.7 14.1 broadcast_multiply_fusion
  127.8 24.3 %mul.98 = f32[28,64,32,64]{3,2,1,0:T(8,128)} reshape(f32[1,1,1792,2048]{3,2,1,0:T(8,128)} %broadcast_multiply_fusion) | data formatting | bytes 29360128 | tf_op jit(solution)/shard_map/mul | solution.py:45
  152.1 0.1 reshape.115
  152.3 0.0 copy-start.4
  152.3 0.0 copy-start.6
  152.3 41.1 %all-to-all-done = bf16[8,2,229376]{2,1,0:T(2,128)(2,1)} async-done(((bf16[8,2,229376]{2,1,0:T(2,128)(2,1)}), bf16[8,2,229376]{2,1,0:T(2,128)(2,1)}, u32[]{:S(2)}, u32[]{:S(2)}) %all-to-all-start) | async-done | bytes 7340064 | tf_op jit(solution)/shard_map/all_to_all | solution.py:42
  193.4 12.1 reshape.131
  205.5 15.9 copy.46
  221.4 21.6 %reshape.112 = f32[28,64,32,64]{3,2,1,0:T(8,128)} reshape(f32[1,1,1792,8,256]{4,3,2,1,0:T(8,128)} %bitcast.47) | data formatting | bytes 29360128 | tf_op jit(solution)/shard_map/convert_element_type | solution.py:47
  243.1 29.9 %add.64 = f32[28,64,32,64]{3,2,1,0:T(8,128)} add(f32[28,64,32,64]{3,2,1,0:T(8,128)} %mul.98, f32[28,64,32,64]{3,2,1,0:T(8,128)} %reshape.112) | non-fusion elementwise | flops 3670016 | bytes 44040192 | tf_op jit(solution)/shard_map/add | solution.py:45
  273.0 53.0 %fusion = f32[28,32,64,64]{2,3,1,0:T(8,128)} fusion(f32[28,64,32,64]{3,2,1,0:T(8,128)} %add.64, f32[64]{0:T(128)S(1)} %get-tuple-element.5, f32[64]{0:T(128)S(1)} %get-tuple-element.4), kind=kOutput, calls=%fused_computation.2 | convolution fusion | flops 2818584576 | bytes 29360640 | tf_op jit(solution)/shard_map/ui,piqj,vj->pquv/dot_general | solution.py:23
  326.0 0.0 copy-done.4
  326.0 0.0 copy-done.6
  326.0 29.6 %fusion.7 = f32[28,32,64,64]{3,2,1,0:T(8,128)} fusion(f32[28,32,64,64]{2,3,1,0:T(8,128)} %fusion, f32[64]{0:T(128)S(1)} %get-tuple-element.5, f32[64]{0:T(128)S(1)} %get-tuple-element.4), kind=kOutput, calls=%fused_computation.21 | convolution fusion | flops 2818584576 | bytes 29360640 | tf_op jit(solution)/shard_map/ui,piqj,vj->pquv/dot_general | solution.py:23
  355.6 24.7 %reshape.101 = f32[28,32,4096]{2,1,0:T(8,128)} reshape(f32[28,32,64,64]{3,2,1,0:T(8,128)} %fusion.7) | data formatting | bytes 29360128 | tf_op jit(solution)/shard_map/reshape | solution.py:51
  380.3 0.0 copy-start.3
  380.3 397.9 %gather_fusion = f32[28672]{0:T(1024)S(1)} fusion(f32[28,32,4096]{2,1,0:T(8,128)} %reshape.101, s32[28672]{0:T(1024)S(1)} %reshape.115), kind=kCustom, calls=%fused_computation | custom fusion | bytes 573440 | tf_op jit(solution)/shard_map/jit(take_along_axis)/gather | solution.py:53
  778.3 0.2 reshape.118
  778.4 0.0 copy-done.3
  778.4 0.1 and_select_fusion
  778.5 0.1 reshape.123
  778.7 156.3 %scatter_custom_fusion = f32[3670016]{0:T(1024)} fusion(s32[28672]{0:T(1024)} %reshape.121, f32[28672]{0:T(1024)S(1)} %reshape.123, f32[]{:T(128)} %constant.15.clone.1), kind=kCustom, calls=%fused_computation.7 | custom fusion | flops 28672 | bytes 14680576
  935.0 0.0 copy-start.5
  935.0 0.0 copy-start.7
  935.0 22.0 %reshape.102 = f32[28,32,64,64]{3,2,1,0:T(8,128)} reshape(f32[3670016]{0:T(1024)} %scatter_custom_fusion) | data formatting | bytes 29360128 | tf_op jit(solution)/shard_map/reshape | solution.py:54
  957.0 0.0 copy-done.5
  957.0 0.0 copy-done.7
  957.0 34.3 %fusion.5 = f32[28,32,64,64]{2,3,1,0:T(8,128)} fusion(f32[28,32,64,64]{3,2,1,0:T(8,128)} %reshape.102, f32[64]{0:T(128)S(1)} %copy-done.7, f32[64]{0:T(128)S(1)} %copy-done.5), kind=kOutput, calls=%fused_computation.19 | convolution fusion | flops 2818584576 | bytes 29360640 | tf_op jit(solution)/shard_map/ui,pquv,vj->piqj/dot_general | solution.py:27
  991.3 29.2 %convolution_bitcast_fusion = f32[28,64,32,64]{3,1,2,0:T(8,128)S(1)} fusion(f32[28,32,64,64]{2,3,1,0:T(8,128)} %fusion.5, f32[64]{0:T(128)S(1)} %copy-done.7, f32[64]{0:T(128)S(1)} %copy-done.5), kind=kOutput, calls=%fused_computation.6 | convolution fusion | flops 2818584576 | bytes 29360640 | tf_op jit(solution)/shard_map/ui,pquv,vj->piqj/dot_general | solution.py:27
  1020.5 19.4 %copy.33 = f32[28,64,32,64]{3,2,1,0:T(8,128)} copy(f32[28,64,32,64]{3,1,2,0:T(8,128)S(1)} %convolution_bitcast_fusion) | data formatting | bytes 29360128 | tf_op jit(solution)/shard_map/ui,pquv,vj->piqj/transpose | solution.py:27
  1039.9 25.4 %broadcast_in_dim.39 = f32[1,1792,2048]{2,1,0:T(8,128)} reshape(f32[28,64,32,64]{3,2,1,0:T(8,128)} %copy.33) | data formatting | bytes 29360128 | tf_op jit(solution)/shard_map/broadcast_in_dim | solution.py:58
  1065.2 0.0 all-reduce.2.cloned.1.call-update
  1065.3 494.7 %all-reduce.2.cloned.1.call-done = f32[1,1792,2048]{2,1,0:T(8,128)} async-done(((f32[1,1792,2048]{2,1,0:T(8,128)}), f32[1,1792,2048]{2,1,0:T(8,128)}) %all-reduce.2.cloned.1.call-update) | async-done | bytes 14680080 | tf_op jit(solution)/shard_map/psum | solution.py:57
  1560.0 32.1 %copy.35 = f32[1,1792,2048]{1,0,2:T(1,128)} copy(f32[1,1792,2048]{2,1,0:T(8,128)} %all-reduce.2.cloned.1.call-done) | data formatting | bytes 29360128 | tf_op jit(solution)/shard_map/psum | solution.py:57
  1592.1 5.6 all-to-all-start.1
  1597.7 25.4 %reshape.103 = f32[1,1,1792,2048]{3,2,1,0:T(8,128)} reshape(f32[28,64,32,64]{3,2,1,0:T(8,128)} %copy.33) | data formatting | bytes 29360128 | tf_op jit(solution)/shard_map/reshape | solution.py:55
  1623.1 15.8 reshape.111
  1638.9 20.9 %add_subtract_fusion = f32[1,1,1792,2048]{3,2,1,0:T(8,128)} fusion(f32[1,1,1792,2048]{3,2,1,0:T(8,128)} %reshape.103, f32[1,1,1792,2048]{3,2,1,0:T(8,128)} %reshape.111, f32[1,1,1792,2048]{3,2,1,0:T(8,128)} %param.4), kind=kLoop, calls=%fused_computation.5 | loop fusion | flops 11010048 | bytes 58720256 | tf_op jit(solution)/shard_map/sub | solution.py:56
  1659.8 99.3 %all-to-all-done.1 = f32[1,1792,2048]{1,0,2:T(1,128)} async-done(((f32[1,1792,2048]{1,0,2:T(1,128)}), f32[1,1792,2048]{1,0,2:T(1,128)}, u32[]{:S(2)}, u32[]{:S(2)}) %all-to-all-start.1) | async-done | bytes 14680096 | tf_op jit(solution)/shard_map/all_to_all | solution.py:58
  1759.1 11.3 copy.41
  1770.5 0.0 copy-start.1
  1770.5 14.4 copy.36
  1784.9 0.0 copy-done.1
  (3 shorter events, 0.1 us)
Async XLA Ops:
  7.2 103.4 %copy-start = (s32[28,32,4,32]{3,2,1,0:T(4,128)S(1)}, s32[28,32,4,32]{3,2,1,0:T(4,128)}, u32[]{:S(2)}) copy-start(s32[28,32,4,32]{3,2,1,0:T(4,128)} %param.5) | copy-start | bytes 1376260
  96.0 16.1 copy-start.9
  96.0 16.4 copy-start.8
  105.1 88.4 %all-to-all-start = ((bf16[8,2,229376]{2,1,0:T(2,128)(2,1)}), bf16[8,2,229376]{2,1,0:T(2,128)(2,1)}, u32[]{:S(2)}, u32[]{:S(2)}) async-start(bf16[8,2,229376]{2,1,0:T(2,128)(2,1)} %reshape.130), calls=%async_computation | async-start | bytes 14680064 | tf_op jit(solution)/shard_map/all_to_all | solution.py:42
  110.3 1449.7 %all-reduce.2.cloned.1.call-start = ((), (), s32[]{:S(2)}) async-start(), calls=%async_computation.2 | async-start | bytes 29360128 | tf_op jit(solution)/shard_map/psum | solution.py:57
  111.1 0.8 copy-start.2
  152.3 173.7 %copy-start.4 = (f32[64]{0:T(128)}, f32[64]{0:T(128)S(1)}, u32[]{:S(2)}) copy-start(f32[64]{0:T(128)S(1)} %get-tuple-element.4) | copy-start | bytes 772
  152.3 173.7 %copy-start.6 = (f32[64]{0:T(128)}, f32[64]{0:T(128)S(1)}, u32[]{:S(2)}) copy-start(f32[64]{0:T(128)S(1)} %get-tuple-element.5) | copy-start | bytes 772
  380.3 398.1 %copy-start.3 = (s32[28,32,1,32]{3,2,1,0:T(1,128)S(1)}, s32[28,32,1,32]{3,2,1,0:T(1,128)}, u32[]{:S(2)}) copy-start(s32[28,32,1,32]{3,2,1,0:T(1,128)} %copy-done.2) | copy-start | bytes 344068
  935.0 22.0 %copy-start.5 = (f32[64]{0:T(128)S(1)}, f32[64]{0:T(128)}, u32[]{:S(2)}) copy-start(f32[64]{0:T(128)} %copy-done.4) | copy-start | bytes 772
  935.0 22.0 %copy-start.7 = (f32[64]{0:T(128)S(1)}, f32[64]{0:T(128)}, u32[]{:S(2)}) copy-start(f32[64]{0:T(128)} %copy-done.6) | copy-start | bytes 772
  1592.1 167.0 %all-to-all-start.1 = ((f32[1,1792,2048]{1,0,2:T(1,128)}), f32[1,1792,2048]{1,0,2:T(1,128)}, u32[]{:S(2)}, u32[]{:S(2)}) async-start(f32[1,1792,2048]{1,0,2:T(1,128)} %copy.35), calls=%async_computation.1 | async-start | bytes 29360128 | tf_op jit(solution)/shard_map/all_to_all | solution.py:58
  1770.5 14.4 copy-start.1
Sparse Core Ops, SparseCore 0:
  1065.4 494.5 all-reduce.1
where the time goes:
time: 1810 us; the launch traced here: 1790 us
  local copies, waits for them, and re-layouts  688 us (38%)
  waiting for transfers between devices  635 us (35%)
  other arithmetic  297 us (16%)
  matrix products  146 us (8%)
    psum x1, waiting for transfers between devices, on_device(): total = lax.psum(restored, 'dp')  495 us
    gather x2, local copies, waits for them, and re-layouts, on_device(): values = jnp.take_along_axis(coeffs, own, axis=2)  398 us
    unnamed x5, other arithmetic  231 us
    all_to_all x1, waiting for transfers between devices, on_device(): lax.all_to_all(total[None], 'expert', split_axis=2, concat_axis=1, tiled=...  99.3 us
    dot_general x2, matrix products, forward(): jnp.einsum('ui,piqj,vj->pquv', cosine, blocks, cosine, precision=HIGHEST_...  82.6 us
    dot_general x2, matrix products, inverse(): jnp.einsum('ui,pquv,vj->piqj', cosine, coeffs, cosine, precision=HIGHEST_...  63.5 us
    convert_element_type x3, local copies, waits for them, and re-layouts, on_device(): decayed = MOMENTUM_DECAY * momentum.reshape(row_count, col_count) + shift...  53.4 us
    unnamed x26, local copies, waits for them, and re-layouts  48.5 us
  transfers between devices with their start and end apart: 3, of which 3 were waited for; matrix products, arithmetic and copies ran while one was open for 6% of the time, Pallas kernels for 0%

commit v1 on v0

v1 whole, which is shorter than its diff:
```python
import functools
import math

import jax
import jax.numpy as jnp
import numpy as np
from jax import lax
from jax.experimental import pallas as pl
from jax.experimental.pallas import tpu as pltpu
from jax.sharding import PartitionSpec as P

SPAN = 64
MOMENTUM_DECAY = 0.999
CHUNK_WEIGHTS = (1, 1, 1, 1)

F32 = jnp.float32
BF16 = jnp.bfloat16
NT = (((1,), (1,)), ((), ()))


def cosine_table():
    u = np.arange(SPAN, dtype=np.float64)[:, None]
    i = np.arange(SPAN, dtype=np.float64)[None, :]
    scale = np.where(u == 0, math.sqrt(1.0 / SPAN), math.sqrt(2.0 / SPAN))
    return (scale * np.cos(math.pi * (2 * i + 1) * u / (2 * SPAN))).astype(np.float32)


def split_np(x):
    high = x.astype(jnp.bfloat16)
    low = (x - high.astype(np.float32)).astype(jnp.bfloat16)
    return high, low


def split(x):
    high = x.astype(BF16)
    return high, (x - high.astype(F32)).astype(BF16)


def dot(a, b):
    return jnp.dot(a, b, preferred_element_type=F32)


def dot_nt(a, b):
    return lax.dot_general(a, b, NT, preferred_element_type=F32)


def one_hot(rows, target):
    ids = lax.broadcasted_iota(jnp.int32, (rows, target.shape[1]), 0)
    return jnp.where(ids == target, 1.0, 0.0).astype(BF16)


def row_kernel(steps, topk, grad_ref, mom_ref, index_ref, table_ref, *rest):
    next_ref, vals_ref = rest[-2:]
    width = mom_ref.shape[1]
    entries = index_ref.shape[-1]
    lane_block = lax.broadcasted_iota(jnp.int32, (SPAN, entries), 1) // topk
    zero = jnp.zeros((SPAN, entries), F32)
    for step in range(steps):
        rows = pl.ds(step * SPAN, SPAN)
        picked = index_ref[0, step : step + 1, :]
        hot = jnp.concatenate(
            [one_hot(SPAN, picked // SPAN), one_hot(SPAN, picked % SPAN)], axis=1
        )
        gathered = dot(table_ref[...], hot)
        p = gathered[:SPAN, :entries] + gathered[SPAN:, :entries]
        qh = gathered[:SPAN, entries:]
        ql = gathered[SPAN:, entries:]
        spread = jnp.concatenate(
            [
                jnp.concatenate(
                    [
                        jnp.where(lane_block == block, qh, zero).astype(BF16),
                        jnp.where(lane_block == block, ql, zero).astype(BF16),
                    ],
                    axis=1,
                )
                for block in range(width // SPAN)
            ],
            axis=0,
        )
        decayed = MOMENTUM_DECAY * mom_ref[rows, :] + grad_ref[0, rows, :].astype(F32)
        dh, dl = split(decayed)
        half = dot(jnp.concatenate([dh, dl], axis=0), spread)
        half = half[:SPAN] + half[SPAN:]
        half = half[:, :entries] + half[:, entries:]
        value = jnp.sum(half * p, axis=0, keepdims=True)
        vals_ref[0, step : step + 1, :] = value
        vh, vl = split(p * value)
        both = jnp.concatenate(
            [jnp.concatenate([vh, vh], axis=1), jnp.concatenate([vl, vl], axis=1)], axis=0
        )
        restored = dot_nt(both, spread)
        next_ref[rows, :] = decayed - (restored[:SPAN] + restored[SPAN:])


def update_kernel(steps, topk, index_ref, vals_ref, right_ref, left_ref, *rest):
    out_ref, s_ref = rest[-2:]
    replicas = index_ref.shape[0]
    entries = index_ref.shape[-1]
    width = out_ref.shape[1]
    per = min(2, width // SPAN)
    lanes = per * topk
    groups = width // SPAN // per
    total = replicas * lanes
    inner = (lax.broadcasted_iota(jnp.int32, (1, total), 1) // topk) % per
    sub = lax.broadcasted_iota(jnp.int32, (SPAN, total), 0)
    for group in range(groups):
        part = slice(group * lanes, (group + 1) * lanes)
        index = jnp.concatenate([index_ref[r, 0, :, part] for r in range(replicas)], axis=1)
        value = jnp.concatenate([vals_ref[r, 0, :, part] for r in range(replicas)], axis=1)
        for step in range(steps):
            picked = index[step : step + 1, :]
            vals = value[step : step + 1, :]
            at = sub == picked // SPAN
            placed = jnp.where(at, vals, 0.0)
            ph, pl_ = split(placed)
            hot = one_hot(per * SPAN, picked % SPAN + SPAN * inner)
            both = dot_nt(jnp.concatenate([ph, pl_], axis=0), hot)
            s_ref[pl.ds(step * SPAN, SPAN), group * per * SPAN : (group + 1) * per * SPAN] = (
                both[:SPAN] + both[SPAN:]
            )
    sh, sl = split(s_ref[...])
    x = dot(sh, right_ref[0]) + dot(sl, right_ref[0]) + dot(sh, right_ref[1])
    xh, xl = split(x)
    for step in range(steps):
        rows = slice(step * SPAN, (step + 1) * SPAN)
        stacked = jnp.concatenate([xh[rows], xl[rows], xh[rows]], axis=0)
        out_ref[pl.ds(step * SPAN, SPAN), :] = dot(left_ref[...], stacked)


def on_device(gradient, momentum, group_index, *, experts, replicas):
    topk = group_index.shape[3]
    block_rows = group_index.shape[0]
    all_cols = momentum.shape[3]
    all_rows = gradient.shape[1] * gradient.shape[2]
    own_rows = momentum.shape[1] * momentum.shape[2]
    width = gradient.shape[3]
    blocks = width // SPAN
    entries = blocks * topk

    table = cosine_table()
    th, tl = split_np(table)
    gather_table = jnp.asarray(np.concatenate([th.T, tl.T], axis=0))
    eye = np.eye(blocks, dtype=np.float32)
    right_table = jnp.asarray(
        np.stack([np.kron(eye, t.astype(np.float32)).astype(jnp.bfloat16) for t in (th, tl)])
    )
    left_table = jnp.asarray(np.concatenate([th.T, th.T, tl.T], axis=1))

    weights = CHUNK_WEIGHTS if block_rows % sum(CHUNK_WEIGHTS) == 0 else (1, 1)
    unit = block_rows // sum(weights)
    counts = [unit * w for w in weights]
    starts = [sum(counts[:c]) for c in range(len(counts))]

    grad = gradient.reshape(experts, own_rows, width)
    mom = momentum.reshape(own_rows, all_cols)
    replica = lax.axis_index("dp")
    arranged = group_index.reshape(block_rows, experts, blocks, replicas, topk)
    arranged = arranged.transpose(3, 1, 0, 2, 4).reshape(replicas, experts, block_rows, entries)
    own_index = lax.dynamic_index_in_dim(arranged, replica, 0, keepdims=False)
    all_index = lax.all_to_all(arranged, "expert", split_axis=1, concat_axis=1, tiled=True)

    next_buf = None
    update_buf = None
    for count, start in zip(counts, starts):
        rows = count * SPAN
        step_rows = unit * SPAN
        per = count // unit
        first = start // unit
        received = lax.all_to_all(
            lax.slice_in_dim(grad, start * SPAN, start * SPAN + rows, axis=1),
            "expert",
            split_axis=0,
            concat_axis=0,
            tiled=True,
        )
        index_part = own_index.reshape(experts * (block_rows // unit), unit, entries)
        stride = block_rows // unit
        args = [received, mom, index_part, gather_table]
        in_specs = [
            pl.BlockSpec((1, step_rows, width), lambda r, e: (e, r, 0)),
            pl.BlockSpec((step_rows, width), lambda r, e, first=first: (first + r, e)),
            pl.BlockSpec(
                (1, unit, entries),
                lambda r, e, first=first, stride=stride: (e * stride + first + r, 0, 0),
            ),
            pl.BlockSpec((2 * SPAN, SPAN), lambda r, e: (0, 0)),
        ]
        aliases = {}
        if next_buf is not None:
            args.append(next_buf)
            in_specs.append(pl.BlockSpec(memory_space=pl.ANY))
            aliases = {len(args) - 1: 0}
        next_buf, vals = pl.pallas_call(
            functools.partial(row_kernel, unit, topk),
            grid=(per, experts),
            in_specs=in_specs,
            out_specs=[
                pl.BlockSpec((step_rows, width), lambda r, e, first=first: (first + r, e)),
                pl.BlockSpec((1, unit, entries), lambda r, e, per=per: (e * per + r, 0, 0)),
            ],
            out_shape=[
                jax.ShapeDtypeStruct((own_rows, all_cols), F32),
                jax.ShapeDtypeStruct((experts * per, unit, entries), F32),
            ],
            input_output_aliases=aliases,
            cost_estimate=pl.CostEstimate(
                flops=count * experts * 3 * 2 * 128 * 256 * 256,
                bytes_accessed=rows * all_cols * 10,
                transcendentals=0,
            ),
            name="rows_part",
        )(*args)
        sent = jnp.broadcast_to(vals[None], (replicas,) + vals.shape)
        sent = sent.reshape(replicas * experts, per * unit, entries)
        got = lax.all_to_all(sent, ("dp", "expert"), split_axis=0, concat_axis=0, tiled=True)
        got = got.reshape(replicas, experts * per, unit, entries)
        all_part = all_index.reshape(replicas, experts * stride, unit, entries)
        args = [all_part, got, right_table, left_table]
        in_specs = [
            pl.BlockSpec(
                (replicas, 1, unit, entries),
                lambda e, r, first=first, stride=stride: (0, e * stride + first + r, 0, 0),
            ),
            pl.BlockSpec(
                (replicas, 1, unit, entries), lambda e, r, per=per: (0, e * per + r, 0, 0)
            ),
            pl.BlockSpec((2, width, width), lambda e, r: (0, 0, 0)),
            pl.BlockSpec((SPAN, 3 * SPAN), lambda e, r: (0, 0)),
        ]
        aliases = {}
        if update_buf is not None:
            args.append(update_buf)
            in_specs.append(pl.BlockSpec(memory_space=pl.ANY))
            aliases = {len(args) - 1: 0}
        update_buf = pl.pallas_call(
            functools.partial(update_kernel, unit, topk),
            grid=(experts, per),
            in_specs=in_specs,
            out_specs=pl.BlockSpec(
                (step_rows, width),
                lambda e, r, first=first, stride=stride: (e * stride + first + r, 0),
            ),
            out_shape=jax.ShapeDtypeStruct((all_rows, width), F32),
            scratch_shapes=[pltpu.VMEM((step_rows, width), F32)],
            input_output_aliases=aliases,
            cost_estimate=pl.CostEstimate(
                flops=count * experts * 5 * 2 * 128 * 256 * 256,
                bytes_accessed=count * experts * SPAN * width * 4,
                transcendentals=0,
            ),
            name="update_part",
        )(*args)
    return next_buf.reshape(momentum.shape), update_buf[None]


def solution(mesh):
    placed = (
        P("dp", None, None, "expert"),
        P("dp", None, "expert", None),
        P("expert", None, None, None),
    )
    body = functools.partial(
        on_device, experts=mesh.shape["expert"], replicas=mesh.shape["dp"]
    )
    return jax.shard_map(
        body,
        mesh=mesh,
        in_specs=placed,
        out_specs=(P("dp", None, "expert", None), P(None, None, "expert")),
        check_vma=False,
    )
```

time: 1810 us -> 249 us (0.14)
  local copies, waits for them, and re-layouts: 688 us -> 14.6 us
  waiting for transfers between devices: 635 us -> 3.28 us
  other arithmetic: 297 us -> 0 us
  matrix products: 146 us -> 0 us
  Pallas kernels: 0 us -> 115 us
  blocking collectives: 0 us -> 82 us
  starting transfers between devices: 11.1 us -> 32.5 us
    psum x1 -> x0, waiting for transfers between devices: 495 us -> none  [on_device(): total = lax.psum(restored, 'dp')]
    gather x2 -> x0, local copies, waits for them, and re-layouts: 398 us -> none  [on_device(): values = jnp.take_along_axis(coeffs, own, axis=2)]
    unnamed x5 -> x0, other arithmetic: 231 us -> none
    dot_general x4 -> x0, matrix products: 146 us -> none  [the longest x2 82.6 us: forward(): jnp.einsum('ui,piqj,vj->pquv', cosine, blocks, cosine, precision=HIGHEST_...]
    all_to_all x2 -> x6, waiting for transfers between devices: 140 us -> 3.28 us  [the longest x1 3.27 us: on_device(): lax.all_to_all(arranged, 'expert', split_axis=1, concat_axis=1, tiled=True)]
    pallas_call x0 -> x8, Pallas kernels: none -> 115 us  [the longest x4 66 us: on_device(): pl.pallas_call(functools.partial(row_kernel, unit, topk), grid=(per, expe...]
    all_to_all x0 -> x3, blocking collectives: none -> 82 us  [on_device(): lax.all_to_all(lax.slice_in_dim(grad, start * SPAN, start * SPAN + rows,...]
    reshape x3 -> x5, local copies, waits for them, and re-layouts: 72.1 us -> 5.4 us  [the longest x1 1.99 us: on_device(): arranged = group_index.reshape(block_rows, experts, blocks, replicas, topk)]
  transfers between devices with their start and end apart: 3 -> 6, of which waited for: 3 -> 1; matrix products, arithmetic and copies ran while one was open for 6% -> 3% of each run, Pallas kernels for 0% -> 41%
where the time goes in v1:
time: 249 us; the launch traced here: 248 us
  Pallas kernels  115 us (46%)
  blocking collectives  82 us (33%)
  starting transfers between devices  32.5 us (13%)
  local copies, waits for them, and re-layouts  14.6 us (6%)
  waiting for transfers between devices  3.28 us (1%)
    all_to_all x3, blocking collectives, on_device(): lax.all_to_all(lax.slice_in_dim(grad, start * SPAN, start * SPAN + rows,...  82 us
    pallas_call x4, Pallas kernels, on_device(): pl.pallas_call(functools.partial(row_kernel, unit, topk), grid=(per, expe...  66 us
    pallas_call x4, Pallas kernels, on_device(): pl.pallas_call(functools.partial(update_kernel, unit, topk), grid=(expert...  48.8 us
    all_to_all x4, starting transfers between devices, on_device(): lax.all_to_all(sent, ('dp', 'expert'), split_axis=0, concat_axis=0, tiled...  23.7 us
    slice x1, local copies, waits for them, and re-layouts, on_device(): lax.slice_in_dim(grad, start * SPAN, start * SPAN + rows, axis=1)  5.74 us
    all_to_all x1, starting transfers between devices, on_device(): lax.all_to_all(arranged, 'expert', split_axis=1, concat_axis=1, tiled=True)  5.2 us
  transfers between devices with their start and end apart: 6, of which 1 were waited for; matrix products, arithmetic and copies ran while one was open for 3% of the time, Pallas kernels for 41%

profile of v1, /device:TPU:0, one launch (start us, length us, event | category | flops | bytes accessed | tf_op | source)
XLA Modules:
  0.0 248.1 jit_solution(12862051294603045179)
XLA Ops:
  0.6 2.0 copy.38
  2.6 0.8 reshape.63
  3.4 1.1 copy.32
  4.5 5.2 %all-to-all-start.4 = ((s32[4,8,28,128]{3,0,2,1:T(4,128)}), s32[4,8,28,128]{3,0,2,1:T(4,128)S(1)}, u32[]{:S(2)}, u32[]{:S(2)}) async-start(s32[4,8,28,128]{3,0,2,1:T(4,128)} %copy.32), calls=%async_computation.4 | async-start | bytes 917504 | tf_op jit(solution)/shard_map/all_to_all | solution.py:161
  9.7 5.7 %fusion = (bf16[8,448,256]{2,1,0:T(8,128)(2,1)}, bf16[8,448,256]{2,1,0:T(8,128)(2,1)}, bf16[8,448,256]{2,1,0:T(8,128)(2,1)S(1)}, bf16[8,448,256]{2,1,0:T(8,128)(2,1)}) fusion(bf16[8,1792,256]{2,1,0:T(8,128)(2,1)} %bitcast.25), kind=kLoop, calls=%fused_computation.2 | loop fusion | bytes 14680064 | tf_op jit(solution)/shard_map/slice | solution.py:171
  15.4 3.3 %all-to-all-done.4 = s32[4,8,28,128]{3,0,2,1:T(4,128)S(1)} async-done(((s32[4,8,28,128]{3,0,2,1:T(4,128)}), s32[4,8,28,128]{3,0,2,1:T(4,128)S(1)}, u32[]{:S(2)}, u32[]{:S(2)}) %all-to-all-start.4) | async-done | bytes 458784 | tf_op jit(solution)/shard_map/all_to_all | solution.py:161
  18.7 0.0 copy-start
  18.7 28.2 %all_to_all.45.grad_ref = bf16[8,448,256]{2,1,0:T(8,128)(2,1)} all-to-all(bf16[8,448,256]{2,1,0:T(8,128)(2,1)} %get-tuple-element.18), channel_id=1, replica_groups=mesh['expert'=8,'dp'=4] {'expert'}, dimensions={0} | all-to-all | bytes 3670016 | tf_op jit(solution)/shard_map/all_to_all | solution.py:170
  46.9 0.0 copy-done
  46.9 26.9 %all_to_all.46.grad_ref = bf16[8,448,256]{2,1,0:T(8,128)(2,1)} all-to-all(bf16[8,448,256]{2,1,0:T(8,128)(2,1)S(1)} %copy-done), channel_id=1, replica_groups=mesh['expert'=8,'dp'=4] {'expert'}, dimensions={0} | all-to-all | bytes 3670016 | tf_op jit(solution)/shard_map/all_to_all | solution.py:170
  73.8 26.9 %all_to_all.47.grad_ref = bf16[8,448,256]{2,1,0:T(8,128)(2,1)} all-to-all(bf16[8,448,256]{2,1,0:T(8,128)(2,1)S(1)} %get-tuple-element.20), channel_id=1, replica_groups=mesh['expert'=8,'dp'=4] {'expert'}, dimensions={0} | all-to-all | bytes 3670016 | tf_op jit(solution)/shard_map/all_to_all | solution.py:170
  100.7 3.6 %all-to-all-start = ((bf16[8,448,256]{2,1,0:T(8,128)(2,1)}), bf16[8,448,256]{2,1,0:T(8,128)(2,1)S(1)}, u32[]{:S(2)}, u32[]{:S(2)}) async-start(bf16[8,448,256]{2,1,0:T(8,128)(2,1)} %get-tuple-element.21), calls=%async_computation | async-start | bytes 3670016 | tf_op jit(solution)/shard_map/all_to_all | solution.py:170
  104.4 0.7 reshape.64.index_ref
  105.0 0.9 copy.36.index_ref
  105.9 16.5 %rows_part.4 = (f32[1792,2048]{1,0:T(8,128)}, f32[8,7,128]{2,1,0:T(8,128)}) custom-call(bf16[8,448,256]{2,1,0:T(8,128)(2,1)} %all_to_all.45.grad_ref, f32[1792,2048]{1,0:T(8,128)} %bitcast.19, s32[32,7,128]{2,1,0:T(8,128)} %reshape.64.index_ref, bf16[128,64]{1,0:T(8,128)(2,1)} %constant.16.clone.table_ref), custom_call_target="tpu_custom_call" | custom-call | flops 2818572288 | bytes 9175040 | tf_op jit(solution)/shard_map/rows_part/pallas_call | solution.py:194
  122.4 16.5 %rows_part.5 = (f32[1792,2048]{1,0:T(8,128)}, f32[8,7,128]{2,1,0:T(8,128)}) custom-call(bf16[8,448,256]{2,1,0:T(8,128)(2,1)} %all_to_all.46.grad_ref, f32[1792,2048]{1,0:T(8,128)} %bitcast.20, s32[32,7,128]{2,1,0:T(8,128)} %reshape.64.index_ref, bf16[128,64]{1,0:T(8,128)(2,1)} %constant.16.clone.table_ref, ...), custom_call_target="tpu_custom_call", output_to_operand_aliasing={{0}: (4, {})} | custom-call | flops 2818572288 | bytes 9175040 | tf_op jit(solution)/shard_map/rows_part/pallas_call | solution.py:194
  138.9 0.0 copy-start.9
  138.9 16.5 %rows_part.6 = (f32[1792,2048]{1,0:T(8,128)}, f32[8,7,128]{2,1,0:T(8,128)}) custom-call(bf16[8,448,256]{2,1,0:T(8,128)(2,1)} %all_to_all.47.grad_ref, f32[1792,2048]{1,0:T(8,128)} %bitcast.21, s32[32,7,128]{2,1,0:T(8,128)} %reshape.64.index_ref, bf16[128,64]{1,0:T(8,128)(2,1)} %constant.16.clone.table_ref, ...), custom_call_target="tpu_custom_call", output_to_operand_aliasing={{0}: (4, {})} | custom-call | flops 2818572288 | bytes 9175040 | tf_op jit(solution)/shard_map/rows_part/pallas_call | solution.py:194
  155.3 0.0 all-to-all-done.grad_ref
  155.3 0.0 copy-start.1
  155.3 0.0 copy-done.9
  155.4 0.7 broadcast_in_dim.13
  156.1 6.2 %all-to-all-start.8 = ((f32[32,7,128]{2,1,0:T(8,128)}), f32[32,7,128]{2,1,0:T(8,128)S(1)}, u32[]{:S(2)}, u32[]{:S(2)}) async-start(f32[32,7,128]{2,1,0:T(8,128)} %bitcast.12), calls=%async_computation.8 | async-start | bytes 262144 | tf_op jit(solution)/shard_map/all_to_all | solution.py:216
  162.3 0.0 copy-done.1
  162.3 0.0 copy-start.8
  162.3 16.6 %rows_part.7 = (f32[1792,2048]{1,0:T(8,128)}, f32[8,7,128]{2,1,0:T(8,128)}) custom-call(bf16[8,448,256]{2,1,0:T(8,128)(2,1)} %copy-done.1, f32[1792,2048]{1,0:T(8,128)} %bitcast.22, s32[32,7,128]{2,1,0:T(8,128)} %reshape.64.index_ref, bf16[128,64]{1,0:T(8,128)(2,1)} %constant.16.clone.table_ref, ...), custom_call_target="tpu_custom_call", output_to_operand_aliasing={{0}: (4, {})} | custom-call | flops 2818572288 | bytes 9175040 | tf_op jit(solution)/shard_map/rows_part/pallas_call | solution.py:194
  178.9 0.0 all-to-all-done.8
  178.9 0.0 copy-start.5
  178.9 0.0 copy-done.8
  179.0 0.7 broadcast_in_dim.12
  179.6 5.8 %all-to-all-start.7 = ((f32[32,7,128]{2,1,0:T(8,128)}), f32[32,7,128]{2,1,0:T(8,128)S(1)}, u32[]{:S(2)}, u32[]{:S(2)}) async-start(f32[32,7,128]{2,1,0:T(8,128)} %bitcast.10), calls=%async_computation.7 | async-start | bytes 262144 | tf_op jit(solution)/shard_map/all_to_all | solution.py:216
  185.5 0.0 copy-done.5
  185.5 0.0 copy-start.6
  185.5 12.2 %update_part.4.rest_0_ = f32[14336,256]{1,0:T(8,128)} custom-call(s32[4,32,7,128]{3,2,1,0:T(8,128)} %copy.36.index_ref, f32[4,8,7,128]{3,2,1,0:T(8,128)} %bitcast.32, bf16[2,256,256]{2,1,0:T(8,128)(2,1)} %constant.17.clone.right_ref, bf16[64,192]{1,0:T(8,128)(2,1)} %constant.18.clone.left_ref), custom_call_target="tpu_custom_call" | custom-call | flops 4697620480 | bytes 3670016 | tf_op jit(solution)/shard_map/update_part/pallas_call | solution.py:236
  197.7 0.0 all-to-all-done.7
  197.7 0.0 copy-start.2
  197.7 0.0 copy-done.6
  197.7 0.7 broadcast_in_dim.11
  198.4 5.8 %all-to-all-start.6 = ((f32[32,7,128]{2,1,0:T(8,128)}), f32[32,7,128]{2,1,0:T(8,128)S(1)}, u32[]{:S(2)}, u32[]{:S(2)}) async-start(f32[32,7,128]{2,1,0:T(8,128)} %bitcast.8), calls=%async_computation.6 | async-start | bytes 262144 | tf_op jit(solution)/shard_map/all_to_all | solution.py:216
  204.2 0.0 copy-done.2
  204.3 0.0 copy-start.7
  204.3 12.2 %update_part.5.rest_0_ = f32[14336,256]{1,0:T(8,128)} custom-call(s32[4,32,7,128]{3,2,1,0:T(8,128)} %copy.36.index_ref, f32[4,8,7,128]{3,2,1,0:T(8,128)} %bitcast.29, bf16[2,256,256]{2,1,0:T(8,128)(2,1)} %constant.17.clone.right_ref, bf16[64,192]{1,0:T(8,128)(2,1)} %constant.18.clone.left_ref, ...), custom_call_target="tpu_custom_call", output_to_operand_aliasing={{}: (4, {})} | custom-call | flops 4697620480 | bytes 3670016 | tf_op jit(solution)/shard_map/update_part/pallas_call | solution.py:236
  216.5 0.0 all-to-all-done.6
  216.5 0.0 copy-start.3
  216.5 0.0 copy-done.7
  216.5 0.7 broadcast_in_dim.10
  217.2 5.8 %all-to-all-start.5 = ((f32[32,7,128]{2,1,0:T(8,128)}), f32[32,7,128]{2,1,0:T(8,128)S(1)}, u32[]{:S(2)}, u32[]{:S(2)}) async-start(f32[32,7,128]{2,1,0:T(8,128)} %bitcast.6), calls=%async_computation.5 | async-start | bytes 262144 | tf_op jit(solution)/shard_map/all_to_all | solution.py:216
  223.0 0.0 copy-done.3
  223.0 12.2 %update_part.6.rest_0_ = f32[14336,256]{1,0:T(8,128)} custom-call(s32[4,32,7,128]{3,2,1,0:T(8,128)} %copy.36.index_ref, f32[4,8,7,128]{3,2,1,0:T(8,128)} %bitcast.30, bf16[2,256,256]{2,1,0:T(8,128)(2,1)} %constant.17.clone.right_ref, bf16[64,192]{1,0:T(8,128)(2,1)} %constant.18.clone.left_ref, ...), custom_call_target="tpu_custom_call", output_to_operand_aliasing={{}: (4, {})} | custom-call | flops 4697620480 | bytes 3670016 | tf_op jit(solution)/shard_map/update_part/pallas_call | solution.py:236
  235.2 0.0 all-to-all-done.5
  235.2 0.0 copy-start.4
  235.3 0.6 copy-done.4
  235.9 12.2 %update_part.7 = f32[14336,256]{1,0:T(8,128)} custom-call(s32[4,32,7,128]{3,2,1,0:T(8,128)} %copy.36.index_ref, f32[4,8,7,128]{3,2,1,0:T(8,128)} %bitcast.31, bf16[2,256,256]{2,1,0:T(8,128)(2,1)} %constant.17.clone.right_ref, bf16[64,192]{1,0:T(8,128)(2,1)} %constant.18.clone.left_ref, f32[14336,256]{1,0:T(8,128)} %update_part.6.rest_0_), custom_call_target="tpu_custom_call", output_to_operand_aliasing={{}: (4, {})} | custom-call | flops 4697620480 | bytes 3670016 | tf_op jit(solution)/shard_map/update_part/pallas_call | solution.py:236
  (2 shorter events, 0.0 us)
Async XLA Ops:
  4.5 14.2 %all-to-all-start.4 = ((s32[4,8,28,128]{3,0,2,1:T(4,128)}), s32[4,8,28,128]{3,0,2,1:T(4,128)S(1)}, u32[]{:S(2)}, u32[]{:S(2)}) async-start(s32[4,8,28,128]{3,0,2,1:T(4,128)} %copy.32), calls=%async_computation.4 | async-start | bytes 917504 | tf_op jit(solution)/shard_map/all_to_all | solution.py:161
  18.7 28.2 %copy-start = (bf16[8,448,256]{2,1,0:T(8,128)(2,1)S(1)}, bf16[8,448,256]{2,1,0:T(8,128)(2,1)}, u32[]{:S(2)}) copy-start(bf16[8,448,256]{2,1,0:T(8,128)(2,1)} %get-tuple-element.19) | copy-start | bytes 5505028
  100.7 54.6 %all-to-all-start = ((bf16[8,448,256]{2,1,0:T(8,128)(2,1)}), bf16[8,448,256]{2,1,0:T(8,128)(2,1)S(1)}, u32[]{:S(2)}, u32[]{:S(2)}) async-start(bf16[8,448,256]{2,1,0:T(8,128)(2,1)} %get-tuple-element.21), calls=%async_computation | async-start | bytes 3670016 | tf_op jit(solution)/shard_map/all_to_all | solution.py:170
  138.9 16.5 %copy-start.9 = (f32[8,7,128]{2,1,0:T(8,128)S(1)}, f32[8,7,128]{2,1,0:T(8,128)}, u32[]{:S(2)}) copy-start(f32[8,7,128]{2,1,0:T(8,128)} %get-tuple-element.17) | copy-start | bytes 86020
  155.3 7.0 %copy-start.1 = (bf16[8,448,256]{2,1,0:T(8,128)(2,1)}, bf16[8,448,256]{2,1,0:T(8,128)(2,1)S(1)}, u32[]{:S(2)}) copy-start(bf16[8,448,256]{2,1,0:T(8,128)(2,1)S(1)} %all-to-all-done.grad_ref) | copy-start | bytes 5505028
  156.1 22.9 %all-to-all-start.8 = ((f32[32,7,128]{2,1,0:T(8,128)}), f32[32,7,128]{2,1,0:T(8,128)S(1)}, u32[]{:S(2)}, u32[]{:S(2)}) async-start(f32[32,7,128]{2,1,0:T(8,128)} %bitcast.12), calls=%async_computation.8 | async-start | bytes 262144 | tf_op jit(solution)/shard_map/all_to_all | solution.py:216
  162.3 16.6 %copy-start.8 = (f32[8,7,128]{2,1,0:T(8,128)S(1)}, f32[8,7,128]{2,1,0:T(8,128)}, u32[]{:S(2)}) copy-start(f32[8,7,128]{2,1,0:T(8,128)} %get-tuple-element.16) | copy-start | bytes 86020
  178.9 6.5 %copy-start.5 = (f32[32,7,128]{2,1,0:T(8,128)}, f32[32,7,128]{2,1,0:T(8,128)S(1)}, u32[]{:S(2)}) copy-start(f32[32,7,128]{2,1,0:T(8,128)S(1)} %all-to-all-done.8) | copy-start | bytes 344068
  179.6 18.1 %all-to-all-start.7 = ((f32[32,7,128]{2,1,0:T(8,128)}), f32[32,7,128]{2,1,0:T(8,128)S(1)}, u32[]{:S(2)}, u32[]{:S(2)}) async-start(f32[32,7,128]{2,1,0:T(8,128)} %bitcast.10), calls=%async_computation.7 | async-start | bytes 262144 | tf_op jit(solution)/shard_map/all_to_all | solution.py:216
  185.5 12.2 %copy-start.6 = (f32[8,7,128]{2,1,0:T(8,128)S(1)}, f32[8,7,128]{2,1,0:T(8,128)}, u32[]{:S(2)}) copy-start(f32[8,7,128]{2,1,0:T(8,128)} %get-tuple-element.15) | copy-start | bytes 86020
  197.7 6.5 %copy-start.2 = (f32[32,7,128]{2,1,0:T(8,128)}, f32[32,7,128]{2,1,0:T(8,128)S(1)}, u32[]{:S(2)}) copy-start(f32[32,7,128]{2,1,0:T(8,128)S(1)} %all-to-all-done.7) | copy-start | bytes 344068
  198.4 18.1 %all-to-all-start.6 = ((f32[32,7,128]{2,1,0:T(8,128)}), f32[32,7,128]{2,1,0:T(8,128)S(1)}, u32[]{:S(2)}, u32[]{:S(2)}) async-start(f32[32,7,128]{2,1,0:T(8,128)} %bitcast.8), calls=%async_computation.6 | async-start | bytes 262144 | tf_op jit(solution)/shard_map/all_to_all | solution.py:216
  204.3 12.2 %copy-start.7 = (f32[8,7,128]{2,1,0:T(8,128)S(1)}, f32[8,7,128]{2,1,0:T(8,128)}, u32[]{:S(2)}) copy-start(f32[8,7,128]{2,1,0:T(8,128)} %get-tuple-element.14) | copy-start | bytes 86020
  216.5 6.5 %copy-start.3 = (f32[32,7,128]{2,1,0:T(8,128)}, f32[32,7,128]{2,1,0:T(8,128)S(1)}, u32[]{:S(2)}) copy-start(f32[32,7,128]{2,1,0:T(8,128)S(1)} %all-to-all-done.6) | copy-start | bytes 344068
  217.2 18.1 %all-to-all-start.5 = ((f32[32,7,128]{2,1,0:T(8,128)}), f32[32,7,128]{2,1,0:T(8,128)S(1)}, u32[]{:S(2)}, u32[]{:S(2)}) async-start(f32[32,7,128]{2,1,0:T(8,128)} %bitcast.6), calls=%async_computation.5 | async-start | bytes 262144 | tf_op jit(solution)/shard_map/all_to_all | solution.py:216
  235.2 0.7 copy-start.4

commit v2 on v0

v2 whole, which is shorter than its diff:
```python
import functools
import math

import jax
import jax.numpy as jnp
import numpy as np
from jax import lax
from jax.experimental import pallas as pl
from jax.experimental.pallas import tpu as pltpu
from jax.sharding import PartitionSpec as P

SPAN = 64
LANES = 128
MOMENTUM_DECAY = 0.999
STEP_BLOCKS = 7

F32 = jnp.float32
BF16 = jnp.bfloat16
NT = (((1,), (1,)), ((), ()))


def cosine_table():
    u = np.arange(SPAN, dtype=np.float64)[:, None]
    i = np.arange(SPAN, dtype=np.float64)[None, :]
    scale = np.where(u == 0, math.sqrt(1.0 / SPAN), math.sqrt(2.0 / SPAN))
    return (scale * np.cos(math.pi * (2 * i + 1) * u / (2 * SPAN))).astype(np.float32)


def split_np(x):
    high = x.astype(jnp.bfloat16)
    low = (x - high.astype(np.float32)).astype(jnp.bfloat16)
    return high, low


def split(x):
    high = x.astype(BF16)
    return high, (x - high.astype(F32)).astype(BF16)


def dot(a, b):
    return jnp.dot(a, b, preferred_element_type=F32)


def dot_nt(a, b):
    return lax.dot_general(a, b, NT, preferred_element_type=F32)


def dot_split(high, low, table_ref):
    return dot(high, table_ref[0]) + dot(low, table_ref[0]) + dot(high, table_ref[1])


def lane_gather(table, lanes):
    index = jnp.broadcast_to(lanes, table.shape)
    return jnp.take_along_axis(table, index, axis=1, mode="promise_in_bounds")


def lane_iota(rows):
    return lax.broadcasted_iota(jnp.int32, (rows, LANES), 1)


def row_kernel(
    topk, where_ref, grad_ref, mom_ref, index_ref, lanes_ref, forward_ref, *rest
):
    next_ref, vals_ref, x_ref = rest[-3:]
    steps = vals_ref.shape[1]
    width = mom_ref.shape[1]
    pair = 2 * topk
    decayed = MOMENTUM_DECAY * mom_ref[...] + grad_ref[...].astype(F32)
    next_ref[...] = decayed
    dh, dl = split(decayed)
    x_ref[...] = dot_split(dh, dl, forward_ref)
    row = lane_iota(1)
    second = (row // topk) % 2
    upper = (row // pair) * SPAN
    for part in range(width // LANES):
        index = index_ref[0, 0, :, part * pair : (part + 1) * pair]
        index = jnp.concatenate([index, index], axis=1)
        cols = slice(part * LANES, (part + 1) * LANES)
        for step in range(steps):
            rows = pl.ds(step * SPAN, SPAN)
            picked = index[step : step + 1, :]
            at_row = picked // SPAN
            at_col = picked % SPAN
            p = lane_gather(lanes_ref[0], at_row)
            chosen = lane_gather(x_ref[rows, cols], at_col + second * SPAN)
            value = jnp.sum(chosen * p, axis=0, keepdims=True)
            vals_ref[0, step : step + 1, part * pair : (part + 1) * pair] = value[:, :pair]
            q = lane_gather(lanes_ref[1], at_col + upper)
            spread = jnp.concatenate(
                [jnp.where(second == 0, q, 0.0), jnp.where(second == 1, q, 0.0)], axis=0
            ).astype(BF16)
            vh, vl = split(p * value)
            restored = dot_nt(jnp.concatenate([vh, vl], axis=0), spread)
            next_ref[rows, cols] = next_ref[rows, cols] - (restored[:SPAN] + restored[SPAN:])


def update_kernel(topk, replicas, where_ref, *refs):
    index_refs = refs[:replicas]
    vals_refs = refs[replicas : 2 * replicas]
    lanes_ref, inverse_ref = refs[2 * replicas : 2 * replicas + 2]
    out_ref, zh_ref, zl_ref = refs[-3:]
    steps = vals_refs[0].shape[1]
    width = out_ref.shape[1]
    pair = 2 * topk
    total = replicas * pair
    inner = (lax.broadcasted_iota(jnp.int32, (1, total), 1) // topk) % 2
    sub = lax.broadcasted_iota(jnp.int32, (LANES, total), 0)
    for part in range(width // LANES):
        lanes = slice(part * pair, (part + 1) * pair)
        cols = slice(part * LANES, (part + 1) * LANES)
        index = jnp.concatenate([r[0, 0, 0, :, lanes] for r in index_refs], axis=1)
        value = jnp.concatenate([r[0, :, lanes] for r in vals_refs], axis=1)
        for step in range(steps):
            picked = index[step : step + 1, :]
            vals = value[step : step + 1, :]
            at_row = picked // SPAN
            p = jnp.concatenate(
                [
                    lane_gather(lanes_ref[0], at_row[:, t : t + LANES])
                    for t in range(0, total, LANES)
                ],
                axis=1,
            )
            vh, vl = split(p * vals)
            hot = jnp.where(sub == picked % SPAN + SPAN * inner, 1.0, 0.0).astype(BF16)
            both = dot_nt(jnp.concatenate([vh, vl], axis=0), hot)
            zh, zl = split(both[:SPAN] + both[SPAN:])
            rows = pl.ds(step * SPAN, SPAN)
            zh_ref[rows, cols] = zh
            zl_ref[rows, cols] = zl
    out_ref[...] = dot_split(zh_ref[...], zl_ref[...], inverse_ref)


def on_device(gradient, momentum, group_index, *, experts, replicas):
    topk = group_index.shape[3]
    block_rows = group_index.shape[0]
    all_cols = momentum.shape[3]
    all_rows = gradient.shape[1] * gradient.shape[2]
    own_rows = momentum.shape[1] * momentum.shape[2]
    width = gradient.shape[3]
    blocks = width // SPAN
    entries = blocks * topk
    unit = STEP_BLOCKS
    units = block_rows // unit
    step_rows = unit * SPAN

    table = cosine_table()
    th, tl = split_np(table)
    wide = lambda a, b: np.concatenate([a.astype(np.float32).T, b.astype(np.float32).T], axis=1)
    lane_tables = jnp.asarray(np.stack([wide(table, table), wide(th, tl)]))
    eye = np.eye(blocks, dtype=np.float32)
    kron = lambda t: np.kron(eye, t.astype(np.float32)).astype(jnp.bfloat16)
    forward_tables = jnp.asarray(np.stack([kron(th.T), kron(tl.T)]))
    inverse_tables = jnp.asarray(np.stack([kron(th), kron(tl)]))

    grad = gradient.reshape(experts, own_rows, width)
    mom = momentum.reshape(own_rows, all_cols)
    me = lax.axis_index("expert")
    replica = lax.axis_index("dp")
    order = sorted(range(experts), key=lambda s: (bin(s >> 1).count("1"), s & 1, s))
    arranged = group_index.reshape(block_rows, experts, blocks, replicas, topk)
    arranged = arranged.transpose(3, 1, 0, 2, 4).reshape(replicas, experts, block_rows, entries)
    received = {}
    for s in order:
        part = lax.dynamic_index_in_dim(grad, me ^ s, 0, keepdims=False)
        if s:
            part = lax.ppermute(part, "expert", [(i, i ^ s) for i in range(experts)])
        received[s] = part
    all_index = lax.all_to_all(arranged, "expert", split_axis=1, concat_axis=1, tiled=True)
    own_tiles = arranged.reshape(replicas, experts * units, unit, entries)
    all_tiles = all_index.reshape(replicas, experts * units, unit, entries)

    next_buf = None
    update_buf = None
    half = experts // 2
    groups = (order[:half], order[half:])
    for group in groups:
        kept = {}
        for s in group:
            where = jnp.stack([me ^ s, replica]).astype(jnp.int32)
            args = [where, received[s], mom, own_tiles, lane_tables, forward_tables]
            in_specs = [
                pl.BlockSpec((step_rows, width), lambda i, w: (i, 0)),
                pl.BlockSpec((step_rows, width), lambda i, w: (i, w[0])),
                pl.BlockSpec(
                    (1, 1, unit, entries), lambda i, w: (w[1], w[0] * units + i, 0, 0)
                ),
                pl.BlockSpec((2, SPAN, LANES), lambda i, w: (0, 0, 0)),
                pl.BlockSpec((2, width, width), lambda i, w: (0, 0, 0)),
            ]
            aliases = {}
            if next_buf is not None:
                args.append(next_buf)
                in_specs.append(pl.BlockSpec(memory_space=pl.ANY))
                aliases = {len(args) - 1: 0}
            next_buf, kept[s] = pl.pallas_call(
                functools.partial(row_kernel, topk),
                grid_spec=pltpu.PrefetchScalarGridSpec(
                    num_scalar_prefetch=1,
                    grid=(units,),
                    in_specs=in_specs,
                    out_specs=[
                        pl.BlockSpec((step_rows, width), lambda i, w: (i, w[0])),
                        pl.BlockSpec((1, unit, entries), lambda i, w: (i, 0, 0)),
                    ],
                    scratch_shapes=[pltpu.VMEM((step_rows, width), F32)],
                ),
                out_shape=[
                    jax.ShapeDtypeStruct((own_rows, all_cols), F32),
                    jax.ShapeDtypeStruct((units, unit, entries), F32),
                ],
                input_output_aliases=aliases,
                cost_estimate=pl.CostEstimate(
                    flops=own_rows * width * 2 * 3000,
                    bytes_accessed=own_rows * width * 10,
                    transcendentals=0,
                ),
                name=f"rows_{s}",
            )(*args)
        zero = jnp.zeros((units, unit, entries), F32)
        by_shift = jnp.stack([kept.get(s, zero) for s in range(experts)])
        by_expert = by_shift[me ^ jnp.arange(experts)]
        sent = jnp.broadcast_to(by_expert[:, None], (experts, replicas) + zero.shape)
        sent = sent.reshape((experts * replicas,) + zero.shape)
        got = lax.all_to_all(sent, ("expert", "dp"), split_axis=0, concat_axis=0, tiled=True)
        got = got.reshape(experts * replicas * units, unit, entries)
        group_of = jnp.array(group, jnp.int32) ^ me
        args = [group_of] + [all_tiles] * replicas + [got] * replicas
        args += [lane_tables, inverse_tables]
        in_specs = [
            pl.BlockSpec(
                (1, 1, 1, unit, entries),
                lambda s, i, w, r=r: (0, r, w[s] * units + i, 0, 0),
            )
            for r in range(replicas)
        ]
        in_specs += [
            pl.BlockSpec(
                (1, unit, entries),
                lambda s, i, w, r=r: ((w[s] * replicas + r) * units + i, 0, 0),
            )
            for r in range(replicas)
        ]
        in_specs += [
            pl.BlockSpec((2, SPAN, LANES), lambda s, i, w: (0, 0, 0)),
            pl.BlockSpec((2, width, width), lambda s, i, w: (0, 0, 0)),
        ]
        args[1 : 1 + replicas] = [all_tiles[None]] * replicas
        aliases = {}
        if update_buf is not None:
            args.append(update_buf)
            in_specs.append(pl.BlockSpec(memory_space=pl.ANY))
            aliases = {len(args) - 1: 0}
        update_buf = pl.pallas_call(
            functools.partial(update_kernel, topk, replicas),
            grid_spec=pltpu.PrefetchScalarGridSpec(
                num_scalar_prefetch=1,
                grid=(len(group), units),
                in_specs=in_specs,
                out_specs=pl.BlockSpec((step_rows, width), lambda s, i, w: (w[s] * units + i, 0)),
                scratch_shapes=[
                    pltpu.VMEM((step_rows, width), BF16),
                    pltpu.VMEM((step_rows, width), BF16),
                ],
            ),
            out_shape=jax.ShapeDtypeStruct((all_rows, width), F32),
            input_output_aliases=aliases,
            cost_estimate=pl.CostEstimate(
                flops=len(group) * own_rows * width * 2 * 4000,
                bytes_accessed=len(group) * own_rows * width * 4,
                transcendentals=0,
            ),
            name=f"update_{len(group)}_{group[0]}",
        )(*args)
    return next_buf.reshape(momentum.shape), update_buf[None]


def solution(mesh):
    placed = (
        P("dp", None, None, "expert"),
        P("dp", None, "expert", None),
        P("expert", None, None, None),
    )
    body = functools.partial(
        on_device, experts=mesh.shape["expert"], replicas=mesh.shape["dp"]
    )
    return jax.shard_map(
        body,
        mesh=mesh,
        in_specs=placed,
        out_specs=(P("dp", None, "expert", None), P(None, None, "expert")),
        check_vma=False,
    )
```

time: 1810 us -> 187 us (0.10)
  local copies, waits for them, and re-layouts: 688 us -> 29.1 us
  waiting for transfers between devices: 635 us -> 20.4 us
  other arithmetic: 297 us -> 3.69 us
  matrix products: 146 us -> 0 us
  Pallas kernels: 0 us -> 108 us
    psum x1 -> x0, waiting for transfers between devices: 495 us -> none  [on_device(): total = lax.psum(restored, 'dp')]
    gather x2, local copies, waits for them, and re-layouts: 398 us -> 1.23 us  [on_device(): by_expert = by_shift[me ^ jnp.arange(experts)]]
    unnamed x5 -> x0, other arithmetic: 231 us -> none
    dot_general x4 -> x0, matrix products: 146 us -> none  [the longest x2 82.6 us: forward(): jnp.einsum('ui,piqj,vj->pquv', cosine, blocks, cosine, precision=HIGHEST_...]
    all_to_all x2 -> x3, waiting for transfers between devices: 140 us -> 0.01 us  [the longest x2 0.01 us: on_device(): lax.all_to_all(sent, ('expert', 'dp'), split_axis=0, concat_axis=0, tiled...]
    pallas_call x0 -> x10, Pallas kernels: none -> 108 us  [the longest x8 62.9 us: on_device(): pl.pallas_call(functools.partial(row_kernel, topk), grid_spec=pltpu.Prefe...]
    reshape x3, local copies, waits for them, and re-layouts: 72.1 us -> 6.74 us  [the longest x2 3.39 us: on_device(): arranged.transpose(3, 1, 0, 2, 4)]
    convert_element_type x3 -> x0, local copies, waits for them, and re-layouts: 53.4 us -> none  [on_device(): decayed = MOMENTUM_DECAY * momentum.reshape(row_count, col_count) + shift...]
  transfers between devices with their start and end apart: 3 -> 10, of which waited for: 3 -> 1; matrix products, arithmetic and copies ran while one was open for 6% -> 13% of each run, Pallas kernels for 0% -> 46%
where the time goes in v2:
time: 187 us; the launch traced here: 186 us
  Pallas kernels  108 us (58%)
  local copies, waits for them, and re-layouts  29.1 us (16%)
  starting transfers between devices  23.6 us (13%)
  waiting for transfers between devices  20.4 us (11%)
  other arithmetic  3.69 us (2%)
    pallas_call x8, Pallas kernels, on_device(): pl.pallas_call(functools.partial(row_kernel, topk), grid_spec=pltpu.Prefe...  62.9 us
    pallas_call x2, Pallas kernels, on_device(): pl.pallas_call(functools.partial(update_kernel, topk, replicas), grid_spe...  45.1 us
    ppermute x7, waiting for transfers between devices, on_device(): part = lax.ppermute(part, 'expert', [(i, i ^ s) for i in range(experts)])  20.4 us
    all_to_all x2, starting transfers between devices, on_device(): lax.all_to_all(sent, ('expert', 'dp'), split_axis=0, concat_axis=0, tiled...  11.5 us
    ppermute x7, starting transfers between devices, on_device(): part = lax.ppermute(part, 'expert', [(i, i ^ s) for i in range(experts)])  6.88 us
    squeeze x1, local copies, waits for them, and re-layouts, on_device(): part = lax.dynamic_index_in_dim(grad, me ^ s, 0, keepdims=False)  5.88 us
    unnamed x24, local copies, waits for them, and re-layouts  5.36 us
    all_to_all x1, starting transfers between devices, on_device(): lax.all_to_all(arranged, 'expert', split_axis=1, concat_axis=1, tiled=True)  5.2 us
  transfers between devices with their start and end apart: 10, of which 1 were waited for; matrix products, arithmetic and copies ran while one was open for 13% of the time, Pallas kernels for 46%

profile of v2, /device:TPU:0, one launch (start us, length us, event | category | flops | bytes accessed | tf_op | source)
XLA Modules:
  0.0 185.5 jit_solution(8745329776701789277)
XLA Ops:
  0.6 0.0 copy-start.5
  0.6 0.0 copy-start
  0.7 3.4 %copy.131 = s32[28,8,4,4,32]{4,2,1,0,3:T(4,128)} copy(s32[28,8,4,4,32]{4,3,2,1,0:T(4,128)} %bitcast.61) | data formatting | bytes 917504 | tf_op jit(solution)/shard_map/reshape | solution.py:161
  4.0 2.3 %reshape.53 = s32[4,8,28,128]{3,1,2,0:T(8,128)S(1)} reshape(s32[4,8,28,4,32]{4,3,1,2,0:T(4,128)} %bitcast.63) | data formatting | bytes 917504 | tf_op jit(solution)/shard_map/reshape | solution.py:162
  6.3 1.1 copy.100
  7.4 5.2 %all-to-all-start = ((s32[4,8,28,128]{3,0,2,1:T(4,128)}), s32[4,8,28,128]{3,0,2,1:T(4,128)S(1)}, u32[]{:S(2)}, u32[]{:S(2)}) async-start(s32[4,8,28,128]{3,0,2,1:T(4,128)} %copy.100), calls=%async_computation | async-start | bytes 917504 | tf_op jit(solution)/shard_map/all_to_all | solution.py:169
  12.6 5.9 %dynamic-slice_bitcast_fusion = (bf16[1792,256]{1,0:T(8,128)(2,1)}, bf16[1792,256]{1,0:T(8,128)(2,1)}, bf16[1792,256]{1,0:T(8,128)(2,1)}, bf16[1792,256]{1,0:T(8...) fusion(bf16[8,1792,256]{2,1,0:T(8,128)(2,1)} %bitcast.64, ...), kind=kLoop, calls=%fused_computation.3 | loop fusion | bytes 14680096 | tf_op jit(solution)/shard_map/jit(dynamic_index_in_dim)/squeeze | solution.py:165
  18.5 0.5 collective-permute-start.6
  19.0 1.6 collective-permute-start.5
  20.6 1.5 collective-permute-start.4
  22.1 0.0 collective-permute-start.3
  22.1 0.7 collective-permute-start.2
  22.8 0.0 copy-done
  22.8 1.7 copy.120
  24.5 3.1 %reshape.74.index_ref = s32[4,32,7,128]{3,2,1,0:T(8,128)} reshape(s32[4,8,28,4,32]{4,3,2,1,0:T(4,128)} %copy.120) | data formatting | bytes 917504 | tf_op jit(solution)/shard_map/reshape;reshape | solution.py:170
  27.6 0.6 pad_add_fusion
  28.2 0.7 pad_add_fusion.2
  28.9 0.6 pad_add_fusion.4
  29.5 0.7 pad_add_fusion.6
  30.2 0.0 copy-done.5
  30.2 0.6 broadcast_xor_fusion.where_ref
  30.7 7.9 %rows_0.1 = (f32[1792,2048]{1,0:T(8,128)}, f32[4,7,128]{2,1,0:T(8,128)}) custom-call(s32[2]{0:T(128)} %get-tuple-element.49.where_ref, bf16[1792,256]{1,0:T(8,128)(2,1)} %get-tuple-element.34.grad_ref, f32[1792,2048]{1,0:T(8,128)} %bitcast.52, s32[4,32,7,128]{3,2,1,0:T(8,128)} %reshape.74.index_ref, f32[2,64,128]{2,1,0:T(8,128)} %constant.58.clone.lanes_ref.refs_8_, ...), custom_call_target="tpu_custom_call" | custom-call | flops 2752512000 | bytes 4587520 | tf_op jit(solution)/shard_map/rows_0/pallas_call | solution.py:196
  38.6 0.0 copy-done.4
  38.6 0.6 broadcast_xor_fusion.1.where_ref
  39.2 0.7 constant_dynamic-update-slice_fusion.13
  39.9 0.0 all-to-all-done
  39.9 0.9 copy.115.refs_0_.refs_1_.refs_2_.refs_3_
  40.8 0.0 collective-permute-done.6.grad_ref
  40.8 2.5 %collective-permute-start.1 = (bf16[1792,256]{1,0:T(8,128)(2,1)S(1)}, bf16[1792,256]{1,0:T(8,128)(2,1)}, u32[]{:S(2)}, u32[]{:S(2)}) collective-permute-start(bf16[1792,256]{1,0:T(8,128)(2,1)S(1)} %copy-done.1), channel_id=1, source_target_pairs={{0,24},{4,28},{8,16},{12,20},{16,8},{20,12},{24,0},{28,4},{1,25},{... | collective-permute-start | bytes 2752520 | tf_op jit(solution)/shard_map/ppermute | solution.py:167
  43.3 7.9 %rows_1.1 = (f32[1792,2048]{1,0:T(8,128)}, f32[4,7,128]{2,1,0:T(8,128)}) custom-call(s32[2]{0:T(128)} %get-tuple-element.48.where_ref, bf16[1792,256]{1,0:T(8,128)(2,1)} %collective-permute-done.6.grad_ref, f32[1792,2048]{1,0:T(8,128)} %bitcast.53, s32[4,32,7,128]{3,2,1,0:T(8,128)} %reshape.74.index_ref, ...), custom_call_target="tpu_custom_call", output_to_operand_aliasing={{0}: (6, {})} | custom-call | flops 2752512000 | bytes 4587520 | tf_op jit(solution)/shard_map/rows_1/pallas_call | solution.py:196
  51.2 0.7 constant_dynamic-update-slice_fusion.12
  51.9 0.0 collective-permute-done.5.grad_ref
  51.9 0.1 collective-permute-start
  52.0 7.9 %rows_2.1 = (f32[1792,2048]{1,0:T(8,128)}, f32[4,7,128]{2,1,0:T(8,128)}) custom-call(s32[2]{0:T(128)} %get-tuple-element.47.where_ref, bf16[1792,256]{1,0:T(8,128)(2,1)} %collective-permute-done.5.grad_ref, f32[1792,2048]{1,0:T(8,128)} %bitcast.54, s32[4,32,7,128]{3,2,1,0:T(8,128)} %reshape.74.index_ref, ...), custom_call_target="tpu_custom_call", output_to_operand_aliasing={{0}: (6, {})} | custom-call | flops 2752512000 | bytes 4587520 | tf_op jit(solution)/shard_map/rows_2/pallas_call | solution.py:196
  59.9 0.7 constant_dynamic-update-slice_fusion.11
  60.6 0.0 collective-permute-done.4.grad_ref
  60.6 7.9 %rows_4.1 = (f32[1792,2048]{1,0:T(8,128)}, f32[4,7,128]{2,1,0:T(8,128)}) custom-call(s32[2]{0:T(128)} %get-tuple-element.46.where_ref, bf16[1792,256]{1,0:T(8,128)(2,1)} %collective-permute-done.4.grad_ref, f32[1792,2048]{1,0:T(8,128)} %bitcast.55, s32[4,32,7,128]{3,2,1,0:T(8,128)} %reshape.74.index_ref, ...), custom_call_target="tpu_custom_call", output_to_operand_aliasing={{0}: (6, {})} | custom-call | flops 2752512000 | bytes 4587520 | tf_op jit(solution)/shard_map/rows_4/pallas_call | solution.py:196
  68.5 0.7 constant_dynamic-update-slice_fusion.9
  69.3 0.6 gather_fusion.1
  69.9 0.8 broadcast_in_dim.7
  70.7 6.2 %all-to-all-start.2 = ((f32[32,4,7,128]{3,1,2,0:T(4,128)}), f32[32,4,7,128]{3,1,2,0:T(4,128)S(1)}, u32[]{:S(2)}, u32[]{:S(2)}) async-start(f32[32,4,7,128]{3,1,2,0:T(4,128)} %bitcast.36), calls=%async_computation.2 | async-start | bytes 917504 | tf_op jit(solution)/shard_map/all_to_all | solution.py:225
  76.9 0.0 collective-permute-done.3.grad_ref
  76.9 7.9 %rows_3.1 = (f32[1792,2048]{1,0:T(8,128)}, f32[4,7,128]{2,1,0:T(8,128)}) custom-call(s32[2]{0:T(128)} %get-tuple-element.45.where_ref, bf16[1792,256]{1,0:T(8,128)(2,1)} %collective-permute-done.3.grad_ref, f32[1792,2048]{1,0:T(8,128)} %bitcast.56, s32[4,32,7,128]{3,2,1,0:T(8,128)} %reshape.74.index_ref, ...), custom_call_target="tpu_custom_call", output_to_operand_aliasing={{0}: (6, {})} | custom-call | flops 2752512000 | bytes 4587520 | tf_op jit(solution)/shard_map/rows_3/pallas_call | solution.py:196
  84.8 0.7 constant_dynamic-update-slice_fusion.4
  85.5 20.4 %collective-permute-done.2.grad_ref = bf16[1792,256]{1,0:T(8,128)(2,1)} collective-permute-done((bf16[1792,256]{1,0:T(8,128)(2,1)}, bf16[1792,256]{1,0:T(8,128)(2,1)}, u32[]{:S(2)}, u32[]{:S(2)}) %collective-permute-start.2) | collective-permute-done | bytes 917536 | tf_op jit(solution)/shard_map/ppermute | solution.py:167
  105.9 7.9 %rows_5.1 = (f32[1792,2048]{1,0:T(8,128)}, f32[4,7,128]{2,1,0:T(8,128)}) custom-call(s32[2]{0:T(128)} %get-tuple-element.44.where_ref, bf16[1792,256]{1,0:T(8,128)(2,1)} %collective-permute-done.2.grad_ref, f32[1792,2048]{1,0:T(8,128)} %bitcast.57, s32[4,32,7,128]{3,2,1,0:T(8,128)} %reshape.74.index_ref, ...), custom_call_target="tpu_custom_call", output_to_operand_aliasing={{0}: (6, {})} | custom-call | flops 2752512000 | bytes 4587520 | tf_op jit(solution)/shard_map/rows_5/pallas_call | solution.py:196
  113.8 0.0 collective-permute-done.1.grad_ref
  113.8 0.0 copy-start.3
  113.8 7.9 %rows_6.1 = (f32[1792,2048]{1,0:T(8,128)}, f32[4,7,128]{2,1,0:T(8,128)}) custom-call(s32[2]{0:T(128)} %get-tuple-element.43.where_ref, bf16[1792,256]{1,0:T(8,128)(2,1)} %collective-permute-done.1.grad_ref, f32[1792,2048]{1,0:T(8,128)} %bitcast.58, s32[4,32,7,128]{3,2,1,0:T(8,128)} %reshape.74.index_ref, ...), custom_call_target="tpu_custom_call", output_to_operand_aliasing={{0}: (6, {})} | custom-call | flops 2752512000 | bytes 4587520 | tf_op jit(solution)/shard_map/rows_6/pallas_call | solution.py:196
  121.7 0.7 constant_dynamic-update-slice_fusion.1
  122.4 0.0 collective-permute-done.grad_ref
  122.4 0.0 copy-start.2
  122.4 0.9 copy-done.2
  123.3 7.9 %rows_7.1 = (f32[1792,2048]{1,0:T(8,128)}, f32[4,7,128]{2,1,0:T(8,128)}) custom-call(s32[2]{0:T(128)} %get-tuple-element.42.where_ref, bf16[1792,256]{1,0:T(8,128)(2,1)} %copy-done.2, f32[1792,2048]{1,0:T(8,128)} %bitcast.59, s32[4,32,7,128]{3,2,1,0:T(8,128)} %reshape.74.index_ref, ...), custom_call_target="tpu_custom_call", output_to_operand_aliasing={{0}: (6, {})} | custom-call | flops 2752512000 | bytes 4587520 | tf_op jit(solution)/shard_map/rows_7/pallas_call | solution.py:196
  131.2 0.7 constant_dynamic-update-slice_fusion
  131.9 0.6 gather_fusion
  132.6 0.0 all-to-all-done.2
  132.6 0.8 broadcast_in_dim.6
  133.4 5.3 %all-to-all-start.1 = ((f32[32,4,7,128]{3,1,2,0:T(4,128)}), f32[32,4,7,128]{3,1,2,0:T(4,128)S(1)}, u32[]{:S(2)}, u32[]{:S(2)}) async-start(f32[32,4,7,128]{3,1,2,0:T(4,128)} %bitcast.30), calls=%async_computation.1 | async-start | bytes 917504 | tf_op jit(solution)/shard_map/all_to_all | solution.py:225
  138.7 0.9 copy.110
  139.6 22.5 %update_4_0.1.refs_10_ = f32[14336,256]{1,0:T(8,128)} custom-call(s32[4]{0:T(128)} %broadcast_xor_fusion.where_ref, s32[1,4,32,7,128]{4,3,2,1,0:T(8,128)} %copy.115.refs_0_.refs_1_.refs_2_.refs_3_, s32[1,4,32,7,128]{4,3,2,1,0:T(8,128)} %copy.115.refs_0_.refs_1_.refs_2_.refs_3_, s32[1,4,32,7,128]{4,3,2,1,0:T(8,128)} %copy.115.refs_0_.refs_1_.refs_2_.refs_3_, ...), custom_call_target="tpu_custom_call" | custom-call | flops 14680064000 | bytes 7340032 | tf_op jit(solution)/shard_map/update_4_0/pallas_call | solution.py:254
  162.1 0.0 all-to-all-done.1
  162.1 0.9 copy.105
  163.0 22.5 %update_4_3.1 = f32[14336,256]{1,0:T(8,128)} custom-call(s32[4]{0:T(128)} %broadcast_xor_fusion.1.where_ref, s32[1,4,32,7,128]{4,3,2,1,0:T(8,128)} %copy.115.refs_0_.refs_1_.refs_2_.refs_3_, s32[1,4,32,7,128]{4,3,2,1,0:T(8,128)} %copy.115.refs_0_.refs_1_.refs_2_.refs_3_, ...), custom_call_target="tpu_custom_call", output_to_operand_aliasing={{}: (11, {})} | custom-call | flops 14680064000 | bytes 7340032 | tf_op jit(solution)/shard_map/update_4_3/pallas_call | solution.py:254
  (13 shorter events, 0.1 us)
Async XLA Ops:
  0.6 29.5 %copy-start.5 = (s32[4]{0:T(128)S(1)}, s32[4]{0:T(128)}, u32[]{:S(2)}) copy-start(s32[4]{0:T(128)} %constant.61.clone) | copy-start | bytes 52
  0.6 22.2 %copy-start = (s32[28,32,4,32]{3,2,1,0:T(4,128)S(1)}, s32[28,32,4,32]{3,2,1,0:T(4,128)}, u32[]{:S(2)}) copy-start(s32[28,32,4,32]{3,2,1,0:T(4,128)} %param.10) | copy-start | bytes 1376260
  7.4 32.5 %all-to-all-start = ((s32[4,8,28,128]{3,0,2,1:T(4,128)}), s32[4,8,28,128]{3,0,2,1:T(4,128)S(1)}, u32[]{:S(2)}, u32[]{:S(2)}) async-start(s32[4,8,28,128]{3,0,2,1:T(4,128)} %copy.100), calls=%async_computation | async-start | bytes 917504 | tf_op jit(solution)/shard_map/all_to_all | solution.py:169
  18.5 20.1 %copy-start.4 = (s32[4]{0:T(128)S(1)}, s32[4]{0:T(128)}, u32[]{:S(2)}) copy-start(s32[4]{0:T(128)} %constant.62.clone) | copy-start | bytes 52
  18.5 22.3 %collective-permute-start.6 = (bf16[1792,256]{1,0:T(8,128)(2,1)}, bf16[1792,256]{1,0:T(8,128)(2,1)}, u32[]{:S(2)}, u32[]{:S(2)}) collective-permute-start(bf16[1792,256]{1,0:T(8,128)(2,1)} %get-tuple-element.35), channel_id=1, source_target_pairs={{0,4},{4,0},{8,12},{12,8},{16,20},{20,16},{24,28},{28,24},{1,5},{5... | collective-permute-start | bytes 2752520 | tf_op jit(solution)/shard_map/ppermute | solution.py:167
  19.0 32.9 %collective-permute-start.5 = (bf16[1792,256]{1,0:T(8,128)(2,1)}, bf16[1792,256]{1,0:T(8,128)(2,1)}, u32[]{:S(2)}, u32[]{:S(2)}) collective-permute-start(bf16[1792,256]{1,0:T(8,128)(2,1)} %get-tuple-element.36), channel_id=1, source_target_pairs={{0,8},{4,12},{8,0},{12,4},{16,24},{20,28},{24,16},{28,20},{1,9},{5... | collective-permute-start | bytes 2752520 | tf_op jit(solution)/shard_map/ppermute | solution.py:167
  20.6 40.0 %collective-permute-start.4 = (bf16[1792,256]{1,0:T(8,128)(2,1)}, bf16[1792,256]{1,0:T(8,128)(2,1)}, u32[]{:S(2)}, u32[]{:S(2)}) collective-permute-start(bf16[1792,256]{1,0:T(8,128)(2,1)} %get-tuple-element.37), channel_id=1, source_target_pairs={{0,16},{4,20},{8,24},{12,28},{16,0},{20,4},{24,8},{28,12},{1,17},{... | collective-permute-start | bytes 2752520 | tf_op jit(solution)/shard_map/ppermute | solution.py:167
  22.1 54.8 %collective-permute-start.3 = (bf16[1792,256]{1,0:T(8,128)(2,1)}, bf16[1792,256]{1,0:T(8,128)(2,1)}, u32[]{:S(2)}, u32[]{:S(2)}) collective-permute-start(bf16[1792,256]{1,0:T(8,128)(2,1)} %get-tuple-element.38), channel_id=1, source_target_pairs={{0,12},{4,8},{8,4},{12,0},{16,28},{20,24},{24,20},{28,16},{1,13},{... | collective-permute-start | bytes 2752520 | tf_op jit(solution)/shard_map/ppermute | solution.py:167
  22.1 83.8 %collective-permute-start.2 = (bf16[1792,256]{1,0:T(8,128)(2,1)}, bf16[1792,256]{1,0:T(8,128)(2,1)}, u32[]{:S(2)}, u32[]{:S(2)}) collective-permute-start(bf16[1792,256]{1,0:T(8,128)(2,1)} %get-tuple-element.39), channel_id=1, source_target_pairs={{0,20},{4,16},{8,28},{12,24},{16,4},{20,0},{24,12},{28,8},{1,21},{... | collective-permute-start | bytes 2752520 | tf_op jit(solution)/shard_map/ppermute | solution.py:167
  24.5 16.3 %copy-start.1 = (bf16[1792,256]{1,0:T(8,128)(2,1)S(1)}, bf16[1792,256]{1,0:T(8,128)(2,1)}, u32[]{:S(2)}) copy-start(bf16[1792,256]{1,0:T(8,128)(2,1)} %get-tuple-element.40) | copy-start | bytes 2752516
  40.8 73.0 %collective-permute-start.1 = (bf16[1792,256]{1,0:T(8,128)(2,1)S(1)}, bf16[1792,256]{1,0:T(8,128)(2,1)}, u32[]{:S(2)}, u32[]{:S(2)}) collective-permute-start(bf16[1792,256]{1,0:T(8,128)(2,1)S(1)} %copy-done.1), channel_id=1, source_target_pairs={{0,24},{4,28},{8,16},{12,20},{16,8},{20,12},{24,0},{28,4},{1,25},{... | collective-permute-start | bytes 2752520 | tf_op jit(solution)/shard_map/ppermute | solution.py:167
  51.9 70.5 %collective-permute-start = (bf16[1792,256]{1,0:T(8,128)(2,1)S(1)}, bf16[1792,256]{1,0:T(8,128)(2,1)S(1)}, u32[]{:S(2)}, u32[]{:S(2)}) collective-permute-start(bf16[1792,256]{1,0:T(8,128)(2,1)S(1)} %get-tuple-element.41), channel_id=1, source_target_pairs={{0,28},{4,24},{8,20},{12,16},{16,12},{20,8},{24,4},{28,0},{1,29},{... | collective-permute-start | bytes 2752520 | tf_op jit(solution)/shard_map/ppermute | solution.py:167
  70.7 61.8 %all-to-all-start.2 = ((f32[32,4,7,128]{3,1,2,0:T(4,128)}), f32[32,4,7,128]{3,1,2,0:T(4,128)S(1)}, u32[]{:S(2)}, u32[]{:S(2)}) async-start(f32[32,4,7,128]{3,1,2,0:T(4,128)} %bitcast.36), calls=%async_computation.2 | async-start | bytes 917504 | tf_op jit(solution)/shard_map/all_to_all | solution.py:225
  113.8 7.9 %copy-start.3 = (f32[4,7,128]{2,1,0:T(8,128)S(1)}, f32[4,7,128]{2,1,0:T(8,128)}, u32[]{:S(2)}) copy-start(f32[4,7,128]{2,1,0:T(8,128)} %get-tuple-element.27) | copy-start | bytes 43012
  122.4 0.9 copy-start.2
  133.4 28.7 %all-to-all-start.1 = ((f32[32,4,7,128]{3,1,2,0:T(4,128)}), f32[32,4,7,128]{3,1,2,0:T(4,128)S(1)}, u32[]{:S(2)}, u32[]{:S(2)}) async-start(f32[32,4,7,128]{3,1,2,0:T(4,128)} %bitcast.30), calls=%async_computation.1 | async-start | bytes 917504 | tf_op jit(solution)/shard_map/all_to_all | solution.py:225
